TPU v7x, 32 devices: a whole 2x2x4 slice. The times are simulated.
32 devices in a mesh: groups: 2 (over y), blk: 16 (over z, x, core).
Axes of the slice: x: 2, y: 2, z: 4, core: 2. Of those that a mesh axis runs over, the one named last changes fastest.
Arguments:
- current_states: float32 [16, 8192], P(None, ('groups', 'blk')), parts along dimension 1, may hold values from -0.5 to 0.5
- next_states: float32 [16, 8192], P(None, ('groups', 'blk')), parts along dimension 1, may hold values from -1 to 1
- next_values: float32 [8192], P(('groups', 'blk')), parts along dimension 0, may hold values from 0 to 2.5
- vol_table: float32 [12, 16], replicated, may hold values from 0.15 to 0.45
- date_index: int32 [1], replicated, may hold values from 0 to 11
- strike: float32 [1], replicated, may hold values from 0.8 to 1.2
Outputs:
- continuation: float32 [8192], P(('groups', 'blk')), parts along dimension 0
- node_value: float32 [8192], P(('groups', 'blk')), parts along dimension 0
There are 2 independent parts, one for each index of `groups`. A program takes and returns all parts, laid end to end along the dimension named above; an argument that names none is the same for every part. Nothing has to cross between parts.
All inputs are finite; a program needn't handle non-finite values.
Results may differ from a plain program's by a relative error of at most 0.00012.
Values sent between devices are 32-bit elements; how exact they have to be, the bound alone decides.
A program may use at most 64 MiB of HBM per device.

v0:
```python
import functools
import math

import jax
import jax.numpy as jnp
from jax import lax
from jax.experimental import pallas as pl
from jax.experimental.pallas import tpu as pltpu
from jax.sharding import PartitionSpec as P

rate_year = 0.05
step_years = 0.1
MESH = pl.DeviceIdType.MESH


def inner_size(count):
    size = 1
    while count % (2 * size) == 0 and (2 * size) ** 2 <= count:
        size *= 2
    return size


def radices(size):
    digits = size.bit_length() - 1
    return (2,) * digits if 2**digits == size else (size,)


def moved(place, offset, size, sign):
    result, unit = 0, 1
    for radix in radices(size):
        digit = (place // unit + sign * (offset // unit % radix) + radix) % radix
        result = result + digit * unit
        unit *= radix
    return result


def digit_count(offset):
    return bin(offset).count("1")


def split3(x):
    high = x.astype(jnp.bfloat16)
    rest = x - high.astype(jnp.float32)
    mid = rest.astype(jnp.bfloat16)
    low = (rest - mid.astype(jnp.float32)).astype(jnp.bfloat16)
    return high, mid, low


def norm_rows(x, first):
    norm = -0.5 * jnp.sum(x * x, axis=0, keepdims=True)
    pieces = [piece.astype(jnp.float32) for piece in split3(norm)]
    row = lax.broadcasted_iota(jnp.int32, (16, x.shape[1]), 0)
    at = 0 if first else 3
    rows = jnp.where((row >= 3 - at) & (row < 6 - at), 1.0, 0.0)
    for number, piece in enumerate(pieces):
        rows = jnp.where(row == at + number, piece, rows)
    return rows.astype(jnp.bfloat16)


def anchor_stack(x):
    high, mid, low = split3(x)
    zero = jnp.zeros_like(high)
    return jnp.concatenate([high, high, high, mid, mid, low, norm_rows(x, True), zero], axis=0)


def target_stack(x):
    high, mid, low = split3(x)
    zero = jnp.zeros_like(high)
    return jnp.concatenate([high, mid, low, high, mid, high, norm_rows(x, False), zero], axis=0)


def kernel(
    inner_count,
    outer_count,
    cur_hbm,
    next_hbm,
    val_hbm,
    vol_hbm,
    date_hbm,
    weighted_ref,
    mass_ref,
    best_ref,
    anc,
    tgt,
    val,
    vol,
    date,
    kmat,
    dens_own,
    dens_in,
    part_own,
    part_in,
    in_sem,
    anc_send,
    anc_recv,
    tgt_send,
    tgt_recv,
    val_send,
    val_recv,
    dens_send,
    dens_recv,
    part_send,
    part_recv,
):
    g, h = inner_count, outer_count
    n = anc.shape[2]
    low_count = min(g, 2)
    me = lax.axis_index("blk")
    outer = me // low_count % h
    low = (me + outer * 2 // h) % low_count
    inner = me // (low_count * h) * low_count + low

    def place(inner_place, outer_place):
        high = inner_place // low_count
        turned = (inner_place + outer_place * 2 // h) % low_count
        return {"blk": (high * h + outer_place) * low_count + turned}

    def inner_peer(q):
        return place(moved(inner, q, g, 1), outer)

    def outer_peer(s, sign=1):
        return place(inner, moved(outer, s, h, sign))

    def owner(q):
        return moved(inner, q, g, -1)

    inner_offsets = list(range(g - 1, 0, -1))
    outer_offsets = sorted(range(1, h), key=lambda s: (-digit_count(s), -s))

    barrier = pltpu.get_barrier_semaphore()
    for q in inner_offsets:
        pl.semaphore_signal(barrier, inc=1, device_id=inner_peer(q), device_id_type=MESH)
    for s in outer_offsets:
        pl.semaphore_signal(barrier, inc=1, device_id=outer_peer(s), device_id_type=MESH)

    loads = [
        pltpu.make_async_copy(src, dst, in_sem.at[number])
        for number, (src, dst) in enumerate(
            [
                (next_hbm, tgt.at[inner]),
                (cur_hbm, anc.at[0]),
                (vol_hbm, vol),
                (date_hbm, date),
                (val_hbm, val.at[inner]),
            ]
        )
    ]
    for load in loads:
        load.start()

    def inner_copies(ref, dst, send, recv):
        return {
            q: pltpu.make_async_remote_copy(
                src_ref=ref,
                dst_ref=dst(q),
                send_sem=send.at[q],
                recv_sem=recv.at[q],
                device_id=inner_peer(q),
                device_id_type=MESH,
            )
            for q in inner_offsets
        }

    tgt_copies = inner_copies(tgt.at[inner], lambda q: tgt.at[inner], tgt_send, tgt_recv)
    val_copies = inner_copies(val.at[inner], lambda q: val.at[inner], val_send, val_recv)
    dens_copies = inner_copies(dens_own, lambda q: dens_in.at[q], dens_send, dens_recv)
    anc_copies = {
        s: pltpu.make_async_remote_copy(
            src_ref=anc.at[0],
            dst_ref=anc.at[s],
            send_sem=anc_send.at[s],
            recv_sem=anc_recv.at[s],
            device_id=outer_peer(s),
            device_id_type=MESH,
        )
        for s in outer_offsets
    }
    part_copies = {
        s: pltpu.make_async_remote_copy(
            src_ref=part_own.at[s],
            dst_ref=part_in.at[s],
            send_sem=part_send.at[s],
            recv_sem=part_recv.at[s],
            device_id=outer_peer(s, -1),
            device_id_type=MESH,
        )
        for s in outer_offsets
    }

    pl.semaphore_wait(barrier, (h - 1) + (g - 1))
    loads[0].wait()
    for q in inner_offsets:
        tgt_copies[q].start()
    loads[1].wait()
    for s in outer_offsets:
        anc_copies[s].start()
    for load in loads[2:]:
        load.wait()
    for q in inner_offsets:
        val_copies[q].start()

    dates, assets = vol.shape
    picked = lax.broadcasted_iota(jnp.int32, (dates, assets), 0) == date[0]
    vol_lanes = jnp.sum(jnp.where(picked, vol[...], 0.0), axis=0, keepdims=True)
    eye = lax.broadcasted_iota(jnp.int32, (assets, assets), 0) == lax.broadcasted_iota(
        jnp.int32, (assets, assets), 1
    )
    vol_row = jnp.sum(jnp.where(eye, vol_lanes, 0.0), axis=1, keepdims=True)
    scale = math.sqrt(math.log2(math.e)) / (vol_row * math.sqrt(step_years))
    drift = (rate_year - 0.5 * vol_row * vol_row) * step_years

    rows, columns = {}, {}
    outer_order = [0] + outer_offsets[::-1]
    near = [q for q in range(g) if q < low_count]
    far = [q for q in range(g) if q >= low_count]

    def block(s, q):
        exponent = jnp.dot(rows[s], columns[q], preferred_element_type=jnp.float32)
        weights = jnp.exp2(exponent)
        kmat[s, :, q * n : (q + 1) * n] = weights
        return jnp.sum(weights.reshape(n // 8, 8, n), axis=0)

    density = {q: jnp.zeros((8, n), jnp.float32) for q in range(g)}
    for part in [near] + [[q] for q in reversed(far)]:
        for q in part:
            if q:
                tgt_copies[q].wait_recv()
            columns[q] = target_stack(tgt[owner(q)] * scale)
        for s in outer_order:
            if s not in rows:
                if s:
                    anc_copies[s].wait_recv()
                rows[s] = jnp.transpose(anchor_stack((anc[s] + drift) * scale))
            for q in part:
                density[q] = density[q] + block(s, q)
        for q in part:
            dens_own[owner(q)] = jnp.sum(density[q], axis=0, keepdims=True)

    for q in inner_offsets:
        dens_copies[q].start()
    best = jnp.max(jnp.exp(anc[0]), axis=0, keepdims=True)
    for q in inner_offsets:
        val_copies[q].wait_recv()
    for q in inner_offsets:
        dens_copies[q].wait_recv()
    worth, inverse = {}, {}
    for q in range(g):
        total = dens_own[owner(q)]
        for p in inner_offsets:
            total = total + dens_in[p, owner(q)]
        inverse[q] = 1.0 / total
        worth[q] = val[owner(q)] / total

    for s in outer_order[::-1]:
        weighted = jnp.zeros((n, 128), jnp.float32)
        mass = jnp.zeros((n, 128), jnp.float32)
        for q in range(g):
            for c in range(0, n, 128):
                tile = kmat[s, :, q * n + c : q * n + c + 128]
                weighted = weighted + tile * worth[q][:, c : c + 128]
                mass = mass + tile * inverse[q][:, c : c + 128]
        part_own[s, 0:1, :] = jnp.sum(jnp.transpose(weighted), axis=0, keepdims=True)
        part_own[s, 1:2, :] = jnp.sum(jnp.transpose(mass), axis=0, keepdims=True)
        if s:
            part_copies[s].start()
    sums = part_own[0]
    for s in outer_offsets[::-1]:
        part_copies[s].wait_recv()
        sums = sums + part_in[s]
    weighted_ref[...] = sums[0]
    mass_ref[...] = sums[1]
    best_ref[...] = best.reshape(n)
    for copies in (anc_copies, tgt_copies, val_copies, dens_copies, part_copies):
        for copy in copies.values():
            copy.wait_send()


def body(count, current_states, next_states, next_values, vol_table, date_index, strike):
    assets, n = current_states.shape
    g = inner_size(count)
    h = count // g
    f32 = jnp.float32
    dma = pltpu.SemaphoreType.DMA
    row = pltpu.VMEM((n,), f32)
    w, m, p = pl.pallas_call(
        functools.partial(kernel, g, h),
        out_shape=(row, row, row),
        in_specs=[pl.BlockSpec(memory_space=pltpu.HBM)] * 5,
        out_specs=(pl.BlockSpec(memory_space=pltpu.VMEM),) * 3,
        scratch_shapes=[
            pltpu.VMEM((h, assets, n), f32),
            pltpu.VMEM((g, assets, n), f32),
            pltpu.VMEM((g, 1, n), f32),
            pltpu.VMEM(vol_table.shape, f32),
            pltpu.SMEM((1,), jnp.int32),
            pltpu.VMEM((h, n, g * n), f32),
            pltpu.VMEM((g, 1, n), f32),
            pltpu.VMEM((g, g, 1, n), f32),
            pltpu.VMEM((h, 2, n), f32),
            pltpu.VMEM((h, 2, n), f32),
            dma((5,)),
            dma((h,)),
            dma((h,)),
            dma((g,)),
            dma((g,)),
            dma((g,)),
            dma((g,)),
            dma((g,)),
            dma((g,)),
            dma((h,)),
            dma((h,)),
        ],
        compiler_params=pltpu.CompilerParams(collective_id=0, has_side_effects=True),
    )(current_states, next_states, next_values.reshape(1, n), vol_table, date_index)
    c = math.exp(-rate_year * step_years) * w / m
    return (c, jnp.maximum(jnp.maximum(p - strike[0], 0.0), c))


def solution(mesh):
    placed = (
        P(None, ("groups", "blk")),
        P(None, ("groups", "blk")),
        P(("groups", "blk")),
        P(),
        P(),
        P(),
    )
    return jax.shard_map(
        functools.partial(body, mesh.shape["blk"]),
        mesh=mesh,
        in_specs=placed,
        out_specs=(P(("groups", "blk")), P(("groups", "blk"))),
        check_vma=False,
    )
```

profile of v0, /device:TPU:0, one launch (start us, length us, event | category | flops | bytes accessed | tf_op | source)
XLA Modules:
  0.0 18.4 jit_solution(16589105285533730084)
XLA Ops:
  1.9 15.9 %shard_map.77 = (f32[256]{0:T(256)S(1)}, f32[256]{0:T(256)S(1)}, f32[256]{0:T(256)S(1)}) custom-call(f32[16,256]{1,0:T(8,128)} %cur_hbm.1, f32[16,256]{1,0:T(8,128)} %next_hbm.1, f32[1,256]{1,0:T(1,128)} %bitcast.3, f32[12,16]{1,0:T(8,128)} %vol_hbm.1, s32[1]{0:T(128)S(6)} %copy.8.date_hbm), custom_call_target="tpu_custom_call" | custom-call | tf_op jit(solution)/shard_map/pallas_call | solution.py:285
  17.8 0.6 %maximum_maximum_fusion = (f32[256]{0:T(256)}, f32[256]{0:T(256)}) fusion(f32[256]{0:T(256)S(1)} %get-tuple-element.7, f32[]{:T(128)} %bitcast.2, f32[256]{0:T(256)S(1)} %get-tuple-element.6, f32[256]{0:T(256)S(1)} %get-tuple-element.5), kind=kLoop, calls=%fused_computation | loop fusion | flops 1280 | bytes 5124 | tf_op jit(solution)/shard_map/max | solution.py:316
where the time goes:
time: 18.6 us; the launch traced here: 18.4 us
  Pallas kernels  15.9 us (85%)
  between operations  1.93 us (10%)
  other arithmetic  0.58 us (3%)
    pallas_call x1, Pallas kernels, body(): pl.pallas_call(functools.partial(kernel, g, h), out_shape=(row, row, row)...  15.9 us
    max x1, other arithmetic, body(): return (c, jnp.maximum(jnp.maximum(p - strike[0], 0.0), c))  0.58 us

commit v1 on v0

v1 whole, which is shorter than its diff:
```python
import functools
import math

import jax
import jax.numpy as jnp
from jax import lax
from jax.experimental import pallas as pl
from jax.experimental.pallas import tpu as pltpu
from jax.sharding import PartitionSpec as P

rate_year = 0.05
step_years = 0.1
MESH = pl.DeviceIdType.MESH


def grid_masks(count):
    digits = count.bit_length() - 1
    assert 2**digits == count
    inner_digits = digits // 2
    inner_units = ([1] + [1 << (digits - k) for k in range(1, inner_digits)])[:inner_digits]
    outer_units = [1 << k for k in range(digits) if 1 << k not in inner_units]
    if inner_units and outer_units:
        outer_units[-1] |= 1

    def span(units):
        masks = [0]
        for unit in units:
            masks += [mask ^ unit for mask in masks]
        return masks

    return span(inner_units), span(outer_units)


def split3(x):
    high = x.astype(jnp.bfloat16)
    rest = x - high.astype(jnp.float32)
    mid = rest.astype(jnp.bfloat16)
    low = (rest - mid.astype(jnp.float32)).astype(jnp.bfloat16)
    return high, mid, low


def norm_rows(x, first):
    norm = -0.5 * jnp.sum(x * x, axis=0, keepdims=True)
    pieces = [piece.astype(jnp.float32) for piece in split3(norm)]
    row = lax.broadcasted_iota(jnp.int32, (16, x.shape[1]), 0)
    at = 0 if first else 3
    rows = jnp.where((row >= 3 - at) & (row < 6 - at), 1.0, 0.0)
    for number, piece in enumerate(pieces):
        rows = jnp.where(row == at + number, piece, rows)
    return rows.astype(jnp.bfloat16)


def anchor_stack(x):
    high, mid, low = split3(x)
    zero = jnp.zeros_like(high)
    return jnp.concatenate([high, high, high, mid, mid, low, norm_rows(x, True), zero], axis=0)


def target_stack(x):
    high, mid, low = split3(x)
    zero = jnp.zeros_like(high)
    return jnp.concatenate([high, mid, low, high, mid, high, norm_rows(x, False), zero], axis=0)


def kernel(
    inner,
    outer,
    cur_hbm,
    next_hbm,
    val_hbm,
    vol_hbm,
    date_hbm,
    weighted_ref,
    mass_ref,
    best_ref,
    anc,
    tgt,
    val,
    vol,
    date,
    rows,
    columns,
    kmat,
    dens_own,
    dens_in,
    part_own,
    part_in,
    in_sem,
    send_sem,
    tgt_recv,
    anc_recv,
    val_recv,
    dens_recv,
    part_recv,
):
    g, h = len(inner), len(outer)
    n = anc.shape[2]
    near = min(g, 2)
    me = lax.axis_index("blk")

    loads = [
        pltpu.make_async_copy(src, dst, in_sem.at[number])
        for number, (src, dst) in enumerate(
            [
                (next_hbm, tgt.at[0]),
                (cur_hbm, anc.at[0]),
                (vol_hbm, vol),
                (date_hbm, date),
                (val_hbm, val.at[0]),
            ]
        )
    ]
    for load in loads:
        load.start()

    barrier = pltpu.get_barrier_semaphore()
    far_first = list(range(g - 1, 0, -1)), list(range(h - 1, 0, -1))
    for masks, offsets in zip((inner, outer), far_first):
        for offset in offsets:
            pl.semaphore_signal(barrier, inc=1, device_id={"blk": me ^ masks[offset]}, device_id_type=MESH)

    def copy(src, dst, send, recv, mask):
        return pltpu.make_async_remote_copy(
            src_ref=src,
            dst_ref=dst,
            send_sem=send,
            recv_sem=recv,
            device_id={"blk": me ^ mask},
            device_id_type=MESH,
        )

    def tgt_sem(q):
        return tgt_recv.at[0 if q < near else 1]

    tgt_copies = {q: copy(tgt.at[0], tgt.at[q], send_sem.at[0], tgt_sem(q), inner[q]) for q in far_first[0]}
    anc_copies = {s: copy(anc.at[0], anc.at[s], send_sem.at[1], anc_recv, outer[s]) for s in far_first[1]}
    val_copies = {q: copy(val.at[0], val.at[q], send_sem.at[2], val_recv, inner[q]) for q in far_first[0]}
    dens_copies = {q: copy(dens_own, dens_in.at[q], send_sem.at[3], dens_recv, inner[q]) for q in far_first[0]}
    part_copies = {s: copy(part_own.at[s], part_in.at[s], send_sem.at[4], part_recv, outer[s]) for s in far_first[1]}

    def several(ref, first, last, send, recv):
        span = ref.at[pl.ds(first, last - first)]
        return copy(span, span, send, recv, 1)

    pl.semaphore_wait(barrier, (h - 1) + (g - 1))
    loads[0].wait()
    for each in tgt_copies.values():
        each.start()
    loads[1].wait()
    for each in anc_copies.values():
        each.start()
    for load in loads[2:]:
        load.wait()
    for each in val_copies.values():
        each.start()

    dates, assets = vol.shape
    picked = lax.broadcasted_iota(jnp.int32, (dates, assets), 0) == date[0]
    vol_lanes = jnp.sum(jnp.where(picked, vol[...], 0.0), axis=0, keepdims=True)
    eye = lax.broadcasted_iota(jnp.int32, (assets, assets), 0) == lax.broadcasted_iota(
        jnp.int32, (assets, assets), 1
    )
    vol_row = jnp.sum(jnp.where(eye, vol_lanes, 0.0), axis=1, keepdims=True)
    scale = math.sqrt(math.log2(math.e)) / (vol_row * math.sqrt(step_years))
    drift = (rate_year - 0.5 * vol_row * vol_row) * step_years

    def take_anchor(s):
        rows[s] = jnp.transpose(anchor_stack((anc[s] + drift) * scale))

    def take_target(q):
        columns[q] = target_stack(tgt[q] * scale)

    def block(s, q):
        exponent = jnp.dot(rows[s], columns[q], preferred_element_type=jnp.float32)
        weights = jnp.exp2(exponent)
        kmat[s, :, q * n : (q + 1) * n] = weights
        return jnp.sum(weights.reshape(n // 8, 8, n), axis=0)

    density = {}
    take_anchor(0)
    take_target(0)
    density[0] = block(0, 0)
    if near > 1:
        several(tgt, 1, 2, send_sem.at[0], tgt_recv.at[0]).wait_recv()
        take_target(1)
        density[1] = block(0, 1)
    if h > 1:
        several(anc, 1, h, send_sem.at[1], anc_recv).wait_recv()
        for s in range(1, h):
            take_anchor(s)
        for s in range(1, h):
            for q in range(near):
                density[q] = density[q] + block(s, q)
    for q in range(near):
        dens_own[q] = jnp.sum(density[q], axis=0, keepdims=True)
    if g > near:
        several(tgt, near, g, send_sem.at[0], tgt_recv.at[1]).wait_recv()
        for q in range(near, g):
            take_target(q)
        for q in range(near, g):
            density[q] = jnp.zeros((8, n), jnp.float32)
        for s in range(h):
            for q in range(near, g):
                density[q] = density[q] + block(s, q)
        for q in range(near, g):
            dens_own[q] = jnp.sum(density[q], axis=0, keepdims=True)

    for each in dens_copies.values():
        each.start()
    best = jnp.max(jnp.exp(anc[0]), axis=0, keepdims=True)
    if g > 1:
        several(val, 1, g, send_sem.at[2], val_recv).wait_recv()
        several(dens_in, 1, g, send_sem.at[3], dens_recv).wait_recv()
    worth, inverse = {}, {}
    for q in range(g):
        total = dens_own[q]
        for p in range(1, g):
            total = total + dens_in[p, q ^ p]
        inverse[q] = 1.0 / total
        worth[q] = val[q] / total

    for s in [*far_first[1], 0]:
        for r in range(0, n, 128):
            weighted = jnp.zeros((128, 128), jnp.float32)
            mass = jnp.zeros((128, 128), jnp.float32)
            for q in range(g):
                for c in range(0, n, 128):
                    tile = kmat[s, r : r + 128, q * n + c : q * n + c + 128]
                    weighted = weighted + tile * worth[q][:, c : c + 128]
                    mass = mass + tile * inverse[q][:, c : c + 128]
            part_own[s, 0:1, r : r + 128] = jnp.sum(jnp.transpose(weighted), axis=0, keepdims=True)
            part_own[s, 1:2, r : r + 128] = jnp.sum(jnp.transpose(mass), axis=0, keepdims=True)
        if s:
            part_copies[s].start()
    sums = part_own[0]
    if h > 1:
        several(part_in, 1, h, send_sem.at[4], part_recv).wait_recv()
    for s in range(1, h):
        sums = sums + part_in[s]
    weighted_ref[...] = sums[0]
    mass_ref[...] = sums[1]
    best_ref[...] = best.reshape(n)
    if g > 1:
        several(tgt, 1, g, send_sem.at[0], tgt_recv.at[0]).wait_send()
        several(val, 1, g, send_sem.at[2], val_recv).wait_send()
        several(dens_in, 1, g, send_sem.at[3], dens_recv).wait_send()
    if h > 1:
        several(anc, 1, h, send_sem.at[1], anc_recv).wait_send()
        several(part_in, 1, h, send_sem.at[4], part_recv).wait_send()


def body(count, current_states, next_states, next_values, vol_table, date_index, strike):
    assets, n = current_states.shape
    inner, outer = grid_masks(count)
    g, h = len(inner), len(outer)
    f32, bf16 = jnp.float32, jnp.bfloat16
    dma = pltpu.SemaphoreType.DMA
    row = pltpu.VMEM((n,), f32)
    w, m, p = pl.pallas_call(
        functools.partial(kernel, inner, outer),
        out_shape=(row, row, row),
        in_specs=[pl.BlockSpec(memory_space=pltpu.HBM)] * 5,
        out_specs=(pl.BlockSpec(memory_space=pltpu.VMEM),) * 3,
        scratch_shapes=[
            pltpu.VMEM((h, assets, n), f32),
            pltpu.VMEM((g, assets, n), f32),
            pltpu.VMEM((g, 1, n), f32),
            pltpu.VMEM(vol_table.shape, f32),
            pltpu.SMEM((1,), jnp.int32),
            pltpu.VMEM((h, n, 8 * assets), bf16),
            pltpu.VMEM((g, 8 * assets, n), bf16),
            pltpu.VMEM((h, n, g * n), f32),
            pltpu.VMEM((g, 1, n), f32),
            pltpu.VMEM((g, g, 1, n), f32),
            pltpu.VMEM((h, 2, n), f32),
            pltpu.VMEM((h, 2, n), f32),
            dma((5,)),
            dma((5,)),
            dma((2,)),
            dma,
            dma,
            dma,
            dma,
        ],
        compiler_params=pltpu.CompilerParams(collective_id=0, has_side_effects=True),
    )(current_states, next_states, next_values.reshape(1, n), vol_table, date_index)
    c = math.exp(-rate_year * step_years) * w / m
    return (c, jnp.maximum(jnp.maximum(p - strike[0], 0.0), c))


def solution(mesh):
    placed = (
        P(None, ("groups", "blk")),
        P(None, ("groups", "blk")),
        P(("groups", "blk")),
        P(),
        P(),
        P(),
    )
    return jax.shard_map(
        functools.partial(body, mesh.shape["blk"]),
        mesh=mesh,
        in_specs=placed,
        out_specs=(P(("groups", "blk")), P(("groups", "blk"))),
        check_vma=False,
    )
```

time: 18.6 us -> 17.9 us (0.962)
  the two profiles are of different devices: /device:TPU:0 before, /device:TPU:1 now
where the time goes in v1:
time: 17.9 us; the launch traced here: 17.8 us
  Pallas kernels  15.3 us (85%)
  between operations  1.93 us (11%)
  other arithmetic  0.58 us (3%)
    pallas_call x1, Pallas kernels, body(): pl.pallas_call(functools.partial(kernel, inner, outer), out_shape=(row, r...  15.3 us
    max x1, other arithmetic, body(): return (c, jnp.maximum(jnp.maximum(p - strike[0], 0.0), c))  0.58 us

profile of v1, /device:TPU:1, one launch (start us, length us, event | category | flops | bytes accessed | tf_op | source)
XLA Modules:
  0.0 17.8 jit_solution(8864012613808275996)
XLA Ops:
  1.9 15.3 %shard_map.77 = (f32[256]{0:T(256)S(1)}, f32[256]{0:T(256)S(1)}, f32[256]{0:T(256)S(1)}) custom-call(f32[16,256]{1,0:T(8,128)} %cur_hbm.1, f32[16,256]{1,0:T(8,128)} %next_hbm.1, f32[1,256]{1,0:T(1,128)} %bitcast.3, f32[12,16]{1,0:T(8,128)} %vol_hbm.1, s32[1]{0:T(128)S(6)} %copy.8.date_hbm), custom_call_target="tpu_custom_call" | custom-call | tf_op jit(solution)/shard_map/pallas_call | solution.py:259
  17.2 0.6 %maximum_maximum_fusion = (f32[256]{0:T(256)}, f32[256]{0:T(256)}) fusion(f32[256]{0:T(256)S(1)} %get-tuple-element.7, f32[]{:T(128)} %bitcast.2, f32[256]{0:T(256)S(1)} %get-tuple-element.6, f32[256]{0:T(256)S(1)} %get-tuple-element.5), kind=kLoop, calls=%fused_computation | loop fusion | flops 1280 | bytes 5124 | tf_op jit(solution)/shard_map/max | solution.py:288

commit v2 on v1

--- a/solution.py
+++ b/solution.py
@@ -29,6 +29,11 @@
         return masks
 
     return span(inner_units), span(outer_units)
+
+
+def reader(place, inner):
+    digits = functools.reduce(lambda a, b: a | b, inner)
+    return (place & digits) == (digits & 1)
 
 
 def split3(x):
@@ -69,15 +74,15 @@
     next_hbm,
     val_hbm,
     vol_hbm,
-    date_hbm,
+    facts_ref,
     weighted_ref,
     mass_ref,
-    best_ref,
+    payoff_ref,
     anc,
     tgt,
     val,
     vol,
-    date,
+    facts,
     rows,
     columns,
     kmat,
@@ -90,6 +95,7 @@
     tgt_recv,
     anc_recv,
     val_recv,
+    facts_recv,
     dens_recv,
     part_recv,
 ):
@@ -105,7 +111,6 @@
                 (next_hbm, tgt.at[0]),
                 (cur_hbm, anc.at[0]),
                 (vol_hbm, vol),
-                (date_hbm, date),
                 (val_hbm, val.at[0]),
             ]
         )
@@ -142,7 +147,15 @@
         span = ref.at[pl.ds(first, last - first)]
         return copy(span, span, send, recv, 1)
 
+    reading = reader(me, inner)
     pl.semaphore_wait(barrier, (h - 1) + (g - 1))
+
+    @pl.when(reading)
+    def _():
+        for q in far_first[0]:
+            copy(facts_ref, facts, send_sem.at[5], facts_recv, inner[q]).start()
+        facts[...] = facts_ref[...]
+
     loads[0].wait()
     for each in tgt_copies.values():
         each.start()
@@ -154,8 +167,16 @@
     for each in val_copies.values():
         each.start()
 
+    if g > 1:
+
+        @pl.when(jnp.logical_not(reading))
+        def _():
+            copy(facts_ref, facts, send_sem.at[5], facts_recv, 1).wait_recv()
+
     dates, assets = vol.shape
-    picked = lax.broadcasted_iota(jnp.int32, (dates, assets), 0) == date[0]
+    date = facts[0:1, 0:1].astype(jnp.int32)
+    strike = facts[0:1, 128:129]
+    picked = lax.broadcasted_iota(jnp.int32, (dates, assets), 0) == date
     vol_lanes = jnp.sum(jnp.where(picked, vol[...], 0.0), axis=0, keepdims=True)
     eye = lax.broadcasted_iota(jnp.int32, (assets, assets), 0) == lax.broadcasted_iota(
         jnp.int32, (assets, assets), 1
@@ -208,6 +229,7 @@
     for each in dens_copies.values():
         each.start()
     best = jnp.max(jnp.exp(anc[0]), axis=0, keepdims=True)
+    payoff = jnp.maximum(best - strike, 0.0)
     if g > 1:
         several(val, 1, g, send_sem.at[2], val_recv).wait_recv()
         several(dens_in, 1, g, send_sem.at[3], dens_recv).wait_recv()
@@ -239,7 +261,7 @@
         sums = sums + part_in[s]
     weighted_ref[...] = sums[0]
     mass_ref[...] = sums[1]
-    best_ref[...] = best.reshape(n)
+    payoff_ref[...] = payoff.reshape(n)
     if g > 1:
         several(tgt, 1, g, send_sem.at[0], tgt_recv.at[0]).wait_send()
         several(val, 1, g, send_sem.at[2], val_recv).wait_send()
@@ -248,6 +270,11 @@
         several(anc, 1, h, send_sem.at[1], anc_recv).wait_send()
         several(part_in, 1, h, send_sem.at[4], part_recv).wait_send()
 
+    @pl.when(reading)
+    def _():
+        for q in far_first[0]:
+            copy(facts_ref, facts, send_sem.at[5], facts_recv, inner[q]).wait_send()
+
 
 def body(count, current_states, next_states, next_values, vol_table, date_index, strike):
     assets, n = current_states.shape
@@ -256,17 +283,24 @@
     f32, bf16 = jnp.float32, jnp.bfloat16
     dma = pltpu.SemaphoreType.DMA
     row = pltpu.VMEM((n,), f32)
+    facts = lax.cond(
+        reader(lax.axis_index("blk"), inner),
+        lambda date, strike: jnp.concatenate([jnp.broadcast_to(date.astype(f32), (128,)), jnp.broadcast_to(strike, (128,))]),
+        lambda date, strike: jnp.zeros((256,), f32),
+        date_index,
+        strike,
+    )
     w, m, p = pl.pallas_call(
         functools.partial(kernel, inner, outer),
         out_shape=(row, row, row),
-        in_specs=[pl.BlockSpec(memory_space=pltpu.HBM)] * 5,
+        in_specs=[pl.BlockSpec(memory_space=pltpu.HBM)] * 4 + [pl.BlockSpec(memory_space=pltpu.VMEM)],
         out_specs=(pl.BlockSpec(memory_space=pltpu.VMEM),) * 3,
         scratch_shapes=[
             pltpu.VMEM((h, assets, n), f32),
             pltpu.VMEM((g, assets, n), f32),
             pltpu.VMEM((g, 1, n), f32),
             pltpu.VMEM(vol_table.shape, f32),
-            pltpu.SMEM((1,), jnp.int32),
+            pltpu.VMEM((1, 256), f32),
             pltpu.VMEM((h, n, 8 * assets), bf16),
             pltpu.VMEM((g, 8 * assets, n), bf16),
             pltpu.VMEM((h, n, g * n), f32),
@@ -274,18 +308,19 @@
             pltpu.VMEM((g, g, 1, n), f32),
             pltpu.VMEM((h, 2, n), f32),
             pltpu.VMEM((h, 2, n), f32),
-            dma((5,)),
-            dma((5,)),
+            dma((4,)),
+            dma((6,)),
             dma((2,)),
+            dma,
             dma,
             dma,
             dma,
             dma,
         ],
         compiler_params=pltpu.CompilerParams(collective_id=0, has_side_effects=True),
-    )(current_states, next_states, next_values.reshape(1, n), vol_table, date_index)
+    )(current_states, next_states, next_values.reshape(1, n), vol_table, facts.reshape(1, 256))
     c = math.exp(-rate_year * step_years) * w / m
-    return (c, jnp.maximum(jnp.maximum(p - strike[0], 0.0), c))
+    return (c, jnp.maximum(p, c))
 
 
 def solution(mesh):

time: 17.9 us -> 16.9 us (0.944)
  between operations: 1.93 us -> 0.65 us
  Pallas kernels: 15.3 us -> 14.2 us
  loops' own time: 0 us -> 0.67 us
  local copies, waits for them, and re-layouts: 0 us -> 0.65 us
    pallas_call x1, Pallas kernels: 15.3 us -> 14.2 us  [body(): pl.pallas_call(functools.partial(kernel, inner, outer), out_shape=(row, r...]
    another operation x0 -> x1, loops' own time: none -> 0.67 us  [body(): lax.cond(reader(lax.axis_index('blk'), inner), lambda date, strike: jnp.c...]
    concatenate x0 -> x1, local copies, waits for them, and re-layouts: none -> 0.65 us  [body(): jnp.concatenate([jnp.broadcast_to(date.astype(f32), (128,)), jnp.broadcas...]
where the time goes in v2:
time: 16.9 us; the launch traced here: 16.7 us
  Pallas kernels  14.2 us (84%)
  loops' own time  0.67 us (4%)
  local copies, waits for them, and re-layouts  0.65 us (4%)
  between operations  0.65 us (4%)
  other arithmetic  0.58 us (3%)
    pallas_call x1, Pallas kernels, body(): pl.pallas_call(functools.partial(kernel, inner, outer), out_shape=(row, r...  14.2 us
    another operation x1, loops' own time, body(): lax.cond(reader(lax.axis_index('blk'), inner), lambda date, strike: jnp.c...  0.67 us
    concatenate x1, local copies, waits for them, and re-layouts, body(): jnp.concatenate([jnp.broadcast_to(date.astype(f32), (128,)), jnp.broadcas...  0.65 us
    max x1, other arithmetic, body(): return (c, jnp.maximum(p, c))  0.58 us

profile of v2, /device:TPU:1, one launch (start us, length us, event | category | flops | bytes accessed | tf_op | source)
XLA Modules:
  0.0 16.7 jit_solution(8853265258560976138)
XLA Ops:
  0.6 1.3 %conditional.1 = (f32[1,256]{1,0:T(1,128)S(1)}) conditional(s32[]{:T(128)} %convert_element_type.6, () %tuple.16, (s32[1]{0:T(128)}, f32[1]{0:T(128)}) %tuple.17), branch_computations={%region_0.0_spmd, %region_1.0_spmd} | conditional | flops 1 | bytes 2072 | solution.py:286
  1.3 0.7 %concatenate.2 = f32[256]{0:T(256)S(1)} pad(f32[128]{0:T(128)S(1)} %broadcast_in_dim.1, f32[]{:T(128)} %bitcast.1), padding=0_128 | pad | bytes 1540 | tf_op jit(solution)/shard_map/cond/branch_1_fun/concatenate | solution.py:288
  2.0 14.2 %shard_map.79 = (f32[256]{0:T(256)S(1)}, f32[256]{0:T(256)S(1)}, f32[256]{0:T(256)S(1)}) custom-call(f32[16,256]{1,0:T(8,128)} %cur_hbm.1, f32[16,256]{1,0:T(8,128)} %next_hbm.1, f32[1,256]{1,0:T(1,128)} %bitcast.4, f32[12,16]{1,0:T(8,128)} %vol_hbm.1, f32[1,256]{1,0:T(1,128)S(1)} %get-tuple-element.24.facts_ref), custom_call_target="tpu_custom_call" | custom-call | tf_op jit(solution)/shard_map/pallas_call | solution.py:293
  16.1 0.6 %fusion = (f32[256]{0:T(256)}, f32[256]{0:T(256)}) fusion(f32[256]{0:T(256)S(1)} %get-tuple-element.17, f32[256]{0:T(256)S(1)} %get-tuple-element.16, f32[256]{0:T(256)S(1)} %get-tuple-element.15), kind=kLoop, calls=%fused_computation.1 | loop fusion | flops 768 | bytes 5120 | tf_op jit(solution)/shard_map/max | solution.py:323
  (1 shorter events, 0.0 us)

commit v3 on v2

--- a/solution.py
+++ b/solution.py
@@ -138,7 +138,7 @@
         return tgt_recv.at[0 if q < near else 1]
 
     tgt_copies = {q: copy(tgt.at[0], tgt.at[q], send_sem.at[0], tgt_sem(q), inner[q]) for q in far_first[0]}
-    anc_copies = {s: copy(anc.at[0], anc.at[s], send_sem.at[1], anc_recv, outer[s]) for s in far_first[1]}
+    anc_copies = {s: copy(anc.at[0], anc.at[s], send_sem.at[1], anc_recv.at[min(s - 1, 1)], outer[s]) for s in far_first[1]}
     val_copies = {q: copy(val.at[0], val.at[q], send_sem.at[2], val_recv, inner[q]) for q in far_first[0]}
     dens_copies = {q: copy(dens_own, dens_in.at[q], send_sem.at[3], dens_recv, inner[q]) for q in far_first[0]}
     part_copies = {s: copy(part_own.at[s], part_in.at[s], send_sem.at[4], part_recv, outer[s]) for s in far_first[1]}
@@ -157,8 +157,14 @@
         facts[...] = facts_ref[...]
 
     loads[0].wait()
-    for each in tgt_copies.values():
-        each.start()
+    def send_far(turn):
+        for pair in range(near, g, 2):
+            q = pair + (me + turn) % 2
+            copy(tgt.at[0], tgt.at[q], send_sem.at[0], tgt_recv.at[1], inner[pair] ^ (me + turn) % 2).start()
+
+    send_far(0)
+    if near > 1:
+        tgt_copies[1].start()
     loads[1].wait()
     for each in anc_copies.values():
         each.start()
@@ -166,6 +172,7 @@
         load.wait()
     for each in val_copies.values():
         each.start()
+    send_far(1)
 
     if g > 1:
 
@@ -197,34 +204,32 @@
         kmat[s, :, q * n : (q + 1) * n] = weights
         return jnp.sum(weights.reshape(n // 8, 8, n), axis=0)
 
-    density = {}
+    first = min(h, 2)
     take_anchor(0)
     take_target(0)
-    density[0] = block(0, 0)
     if near > 1:
         several(tgt, 1, 2, send_sem.at[0], tgt_recv.at[0]).wait_recv()
         take_target(1)
-        density[1] = block(0, 1)
+    density = {q: block(0, q) for q in range(near)}
     if h > 1:
-        several(anc, 1, h, send_sem.at[1], anc_recv).wait_recv()
-        for s in range(1, h):
-            take_anchor(s)
-        for s in range(1, h):
-            for q in range(near):
-                density[q] = density[q] + block(s, q)
-    for q in range(near):
-        dens_own[q] = jnp.sum(density[q], axis=0, keepdims=True)
+        several(anc, 1, 2, send_sem.at[1], anc_recv.at[0]).wait_recv()
+        take_anchor(1)
+        for q in range(near):
+            density[q] = density[q] + block(1, q)
     if g > near:
         several(tgt, near, g, send_sem.at[0], tgt_recv.at[1]).wait_recv()
-        for q in range(near, g):
-            take_target(q)
-        for q in range(near, g):
-            density[q] = jnp.zeros((8, n), jnp.float32)
-        for s in range(h):
-            for q in range(near, g):
-                density[q] = density[q] + block(s, q)
-        for q in range(near, g):
-            dens_own[q] = jnp.sum(density[q], axis=0, keepdims=True)
+    if h > first:
+        several(anc, first, h, send_sem.at[1], anc_recv.at[1]).wait_recv()
+    for q in range(near, g):
+        take_target(q)
+        density[q] = jnp.zeros((8, n), jnp.float32)
+    for s in range(first, h):
+        take_anchor(s)
+    for s in range(h):
+        for q in range(near if s < first else 0, g):
+            density[q] = density[q] + block(s, q)
+    for q in range(g):
+        dens_own[q] = jnp.sum(density[q], axis=0, keepdims=True)
 
     for each in dens_copies.values():
         each.start()
@@ -267,7 +272,7 @@
         several(val, 1, g, send_sem.at[2], val_recv).wait_send()
         several(dens_in, 1, g, send_sem.at[3], dens_recv).wait_send()
     if h > 1:
-        several(anc, 1, h, send_sem.at[1], anc_recv).wait_send()
+        several(anc, 1, h, send_sem.at[1], anc_recv.at[0]).wait_send()
         several(part_in, 1, h, send_sem.at[4], part_recv).wait_send()
 
     @pl.when(reading)
@@ -311,7 +316,7 @@
             dma((4,)),
             dma((6,)),
             dma((2,)),
-            dma,
+            dma((2,)),
             dma,
             dma,
             dma,

time: 16.9 us -> 16.6 us (0.982)
  Pallas kernels: 14.2 us -> 13.9 us
    pallas_call x1, Pallas kernels: 14.2 us -> 13.9 us  [body(): pl.pallas_call(functools.partial(kernel, inner, outer), out_shape=(row, r...]
where the time goes in v3:
time: 16.6 us; the launch traced here: 16.4 us
  Pallas kernels  13.9 us (84%)
  loops' own time  0.67 us (4%)
  local copies, waits for them, and re-layouts  0.65 us (4%)
  between operations  0.65 us (4%)
  other arithmetic  0.58 us (3%)
    pallas_call x1, Pallas kernels, body(): pl.pallas_call(functools.partial(kernel, inner, outer), out_shape=(row, r...  13.9 us
    another operation x1, loops' own time, body(): lax.cond(reader(lax.axis_index('blk'), inner), lambda date, strike: jnp.c...  0.67 us
    concatenate x1, local copies, waits for them, and re-layouts, body(): jnp.concatenate([jnp.broadcast_to(date.astype(f32), (128,)), jnp.broadcas...  0.65 us
    max x1, other arithmetic, body(): return (c, jnp.maximum(p, c))  0.58 us

profile of v3, /device:TPU:1, one launch (start us, length us, event | category | flops | bytes accessed | tf_op | source)
XLA Modules:
  0.0 16.4 jit_solution(16316534321947822738)
XLA Ops:
  0.6 1.3 %conditional.1 = (f32[1,256]{1,0:T(1,128)S(1)}) conditional(s32[]{:T(128)} %convert_element_type.6, () %tuple.16, (s32[1]{0:T(128)}, f32[1]{0:T(128)}) %tuple.17), branch_computations={%region_0.0_spmd, %region_1.0_spmd} | conditional | flops 1 | bytes 2072 | solution.py:291
  1.3 0.7 %concatenate.2 = f32[256]{0:T(256)S(1)} pad(f32[128]{0:T(128)S(1)} %broadcast_in_dim.1, f32[]{:T(128)} %bitcast.1), padding=0_128 | pad | bytes 1540 | tf_op jit(solution)/shard_map/cond/branch_1_fun/concatenate | solution.py:293
  2.0 13.9 %shard_map.79 = (f32[256]{0:T(256)S(1)}, f32[256]{0:T(256)S(1)}, f32[256]{0:T(256)S(1)}) custom-call(f32[16,256]{1,0:T(8,128)} %cur_hbm.1, f32[16,256]{1,0:T(8,128)} %next_hbm.1, f32[1,256]{1,0:T(1,128)} %bitcast.4, f32[12,16]{1,0:T(8,128)} %vol_hbm.1, f32[1,256]{1,0:T(1,128)S(1)} %get-tuple-element.24.facts_ref), custom_call_target="tpu_custom_call" | custom-call | tf_op jit(solution)/shard_map/pallas_call | solution.py:298
  15.9 0.6 %fusion = (f32[256]{0:T(256)}, f32[256]{0:T(256)}) fusion(f32[256]{0:T(256)S(1)} %get-tuple-element.17, f32[256]{0:T(256)S(1)} %get-tuple-element.16, f32[256]{0:T(256)S(1)} %get-tuple-element.15), kind=kLoop, calls=%fused_computation.1 | loop fusion | flops 768 | bytes 5120 | tf_op jit(solution)/shard_map/max | solution.py:328
  (1 shorter events, 0.0 us)
